TPU v7x, 32 devices: a whole 2x2x4 slice. The times are simulated.
32 devices in a mesh: groups: 2 (over y), kvb: 4 (over z), tp: 4 (over x, core).
Axes of the slice: x: 2, y: 2, z: 4, core: 2. Of those that a mesh axis runs over, the one named last changes fastest.
Arguments:
- residual: bfloat16 [32, 8192], P(('groups', 'kvb')), parts along dimension 0, may hold values from -3 to 3
- queries: bfloat16 [32, 8192], P(('groups', 'kvb'), 'tp'), parts along dimension 0, may hold values from -60 to 60
- new_kv: bfloat16 [32, 2048], P(('groups', 'kvb')), parts along dimension 0, may hold values from -6 to 6
- kv_cache: bfloat16 [2048, 16, 2048], P(('groups', 'kvb', 'tp')), parts along dimension 0, may hold values from -6 to 6
- lengths: int32 [32], P('groups'), parts along dimension 0, may hold values from 1 to 2048, as said below
- slot_seq: int32 [2048], P(('groups', 'kvb', 'tp')), parts along dimension 0, may hold values from 0 to 15, as said below
- slot_block: int32 [2048], P(('groups', 'kvb', 'tp')), parts along dimension 0, may hold values from 0 to 127, as said below
- block_counts: int32 [32], P(('groups', 'kvb', 'tp')), parts along dimension 0, may hold values from 16 to 64, as said below
- out_weight: bfloat16 [8192, 8192], P('tp'), may hold values from -0.5 to 0.5
- norm_gain: bfloat16 [8192], P('tp'), may hold values from 0.099609375 to 1.8984375
Outputs:
- stream: bfloat16 [32, 8192], P(('groups', 'kvb'), 'tp'), parts along dimension 0
- normed: bfloat16 [32, 8192], P(('groups', 'kvb'), 'tp'), parts along dimension 0
There are 2 independent parts, one for each index of `groups`. A program takes and returns all parts, laid end to end along the dimension named above; an argument that names none is the same for every part. Nothing has to cross between parts.
Inputs may be any that keep to these rules, and one draw needn't show every extreme that they name: `block_counts`: slots below a device's count hold cache blocks, those at or beyond it none; at least one device's count is 64. `slot_seq`: each pair of a sequence s and a block b below ceil(lengths[s] / 16) sits in exactly one live slot of the group. `slot_block`: some sequence has exactly 128 blocks; none has more. `lengths`: some sequence has exactly 16 * (128) tokens.
All inputs are finite; a program needn't handle non-finite values.
Results may differ from a plain program's by a relative error of at most 0.006.
Values may be sent and summed in bfloat16 or wider, within the bound.
No kernel may reach another device: no remote copies, remote signals or barrier semaphores. Data moves between devices by JAX's collectives and lax.ppermute only.
A program may use at most 64 MiB of HBM per device.

v0:
```python
import jax
import jax.numpy as jnp
from jax import lax
from jax.sharding import PartitionSpec as P

QH = 64
KVH = 8
HD = 128
BLK = 16
NEGATIVE = -1e30
EPSILON = 1e-06


def on_device(
    residual,
    queries,
    new_kv,
    kv_cache,
    lengths,
    slot_seq,
    slot_block,
    block_counts,
    out_weight,
    norm_gain,
):
    tp_count = lax.axis_size("tp")
    kvb_count = lax.axis_size("kvb")
    tp_index = lax.axis_index("tp")
    seq_rep = residual.shape[0]
    local_heads = queries.shape[1] // HD
    group_size = QH // KVH
    score_scale = HD ** (-0.5)
    wide = lax.all_gather(queries, "tp", axis=1, tiled=True)
    every = lax.all_gather(wide, "kvb", axis=0, tiled=True)
    seq_total = every.shape[0]
    grouped = every.reshape(seq_total, KVH, group_size, HD)
    pool_size = kv_cache.shape[0]
    step_slots = min(32, pool_size)
    live_count = block_counts[0]
    seq_ids = jnp.arange(seq_total, dtype=jnp.int32)
    offsets = jnp.arange(BLK, dtype=jnp.int32)

    def advance(turn_index, carried):
        peak_now, weight_sum, partial_rows = carried
        first_slot = turn_index * step_slots
        cache_part = lax.dynamic_slice_in_dim(kv_cache, first_slot, step_slots, 0)
        seq_part = lax.dynamic_slice_in_dim(slot_seq, first_slot, step_slots, 0)
        block_part = lax.dynamic_slice_in_dim(slot_block, first_slot, step_slots, 0)
        key_rows = cache_part[:, :, : KVH * HD].reshape(step_slots * BLK, KVH, HD)
        value_rows = cache_part[:, :, KVH * HD :].reshape(step_slots * BLK, KVH, HD)
        token_seq = jnp.repeat(seq_part, BLK)
        position = (block_part[:, None] * BLK + offsets[None, :]).reshape(-1)
        slot_live = jnp.repeat(
            first_slot + jnp.arange(step_slots, dtype=jnp.int32) < live_count, BLK
        )
        member = token_seq[None, :] == seq_ids[:, None]
        length_of = jnp.sum(jnp.where(member, lengths[:, None], 0), axis=0)
        live = member & (position < length_of)[None, :] & slot_live[None, :]
        mask = live[:, None, None, :]
        scores = (
            jnp.einsum("sgqd,ngd->sgqn", grouped, key_rows, preferred_element_type=jnp.float32)
            * score_scale
        )
        peak_next = jnp.maximum(peak_now, jnp.max(jnp.where(mask, scores, NEGATIVE), axis=-1))
        weights = jnp.where(mask, jnp.exp(scores - peak_next[..., None]), 0.0)
        shrink = jnp.exp(peak_now - peak_next)
        weight_sum = weight_sum * shrink + jnp.sum(weights, axis=-1)
        partial_rows = partial_rows * shrink[..., None] + jnp.einsum(
            "sgqn,ngd->sgqd",
            weights.astype(jnp.bfloat16),
            value_rows,
            preferred_element_type=jnp.float32,
        )
        return (peak_next, weight_sum, partial_rows)

    start_state = (
        jnp.full((seq_total, KVH, group_size), NEGATIVE, jnp.float32),
        jnp.zeros((seq_total, KVH, group_size), jnp.float32),
        jnp.zeros((seq_total, KVH, group_size, HD), jnp.float32),
    )
    turn_count = (live_count + step_slots - 1) // step_slots
    peak_now, weight_sum, partial_rows = lax.fori_loop(0, turn_count, advance, start_state)
    row_out = partial_rows.reshape(kvb_count, seq_rep, tp_count, local_heads * HD).transpose(
        0, 2, 1, 3
    )
    peak_out = peak_now.reshape(kvb_count, seq_rep, tp_count, local_heads).transpose(0, 2, 1, 3)
    sum_out = weight_sum.reshape(kvb_count, seq_rep, tp_count, local_heads).transpose(0, 2, 1, 3)
    device_total = kvb_count * tp_count
    got_rows, got_peaks, got_sums = (
        lax.all_to_all(
            row_out.reshape(device_total, seq_rep, local_heads * HD),
            ("kvb", "tp"),
            split_axis=0,
            concat_axis=0,
            tiled=True,
        ),
        lax.all_to_all(
            peak_out.reshape(device_total, seq_rep, local_heads),
            ("kvb", "tp"),
            split_axis=0,
            concat_axis=0,
            tiled=True,
        ),
        lax.all_to_all(
            sum_out.reshape(device_total, seq_rep, local_heads),
            ("kvb", "tp"),
            split_axis=0,
            concat_axis=0,
            tiled=True,
        ),
    )
    got_rows = got_rows.reshape(device_total, seq_rep, local_heads, HD)
    kv_local = max(1, local_heads // group_size)
    per_kv = local_heads // kv_local
    kv_first = tp_index * local_heads // group_size
    new_keys = lax.dynamic_slice_in_dim(new_kv, kv_first * HD, kv_local * HD, 1).reshape(
        seq_rep, kv_local, HD
    )
    new_values = lax.dynamic_slice_in_dim(new_kv, KVH * HD + kv_first * HD, kv_local * HD, 1)
    new_values = new_values.reshape(seq_rep, kv_local, 1, HD).astype(jnp.float32)
    own_view = queries.reshape(seq_rep, kv_local, per_kv, HD)
    fresh = (
        jnp.einsum("rkqd,rkd->rkq", own_view, new_keys, preferred_element_type=jnp.float32)
        * score_scale
    )
    fresh = fresh.reshape(seq_rep, local_heads)
    fresh_values = jnp.broadcast_to(new_values, (seq_rep, kv_local, per_kv, HD)).reshape(
        seq_rep, local_heads, HD
    )
    overall = jnp.maximum(jnp.max(got_peaks, axis=0), fresh)
    scaling = jnp.exp(got_peaks - overall[None])
    fresh_weight = jnp.exp(fresh - overall)
    denominator = jnp.sum(scaling * got_sums, axis=0) + fresh_weight
    numerator = (
        jnp.sum(scaling[..., None] * got_rows, axis=0) + fresh_weight[..., None] * fresh_values
    )
    attended = (
        (numerator / denominator[..., None]).reshape(seq_rep, local_heads * HD).astype(jnp.bfloat16)
    )
    projected = jnp.dot(attended, out_weight, preferred_element_type=jnp.float32)
    width_dev = norm_gain.shape[0]
    column = tp_index * width_dev
    summed = lax.psum(projected, "tp")
    full_stream = (residual.astype(jnp.float32) + summed).astype(jnp.bfloat16)
    full_wide = lax.optimization_barrier(full_stream).astype(jnp.float32)
    mean_square = jnp.mean(full_wide * full_wide, axis=1)
    stream = lax.dynamic_slice_in_dim(full_stream, column, width_dev, 1)
    stream_wide = lax.dynamic_slice_in_dim(full_wide, column, width_dev, 1)
    normed = (
        stream_wide * lax.rsqrt(mean_square + EPSILON)[:, None] * norm_gain.astype(jnp.float32)
    ).astype(jnp.bfloat16)
    return (stream, normed)


def solution(mesh):
    placed = (
        P(("groups", "kvb"), None),
        P(("groups", "kvb"), "tp"),
        P(("groups", "kvb"), None),
        P(("groups", "kvb", "tp"), None, None),
        P("groups"),
        P(("groups", "kvb", "tp")),
        P(("groups", "kvb", "tp")),
        P(("groups", "kvb", "tp")),
        P("tp", None),
        P("tp"),
    )
    return jax.shard_map(
        on_device,
        mesh=mesh,
        in_specs=placed,
        out_specs=(P(("groups", "kvb"), "tp"), P(("groups", "kvb"), "tp")),
        check_vma=False,
    )
```

profile of v0, /device:TPU:0, one launch (start us, length us, event | category | flops | bytes accessed | tf_op | source)
XLA Modules:
  0.0 138.4 jit_solution(4578274907591061050)
XLA Ops:
  7.8 6.5 %all_gather.6 = bf16[4,8192]{1,0:T(4,128)(2,1)S(1)} all-gather(bf16[4,2048]{1,0:T(4,128)(2,1)} %param.13), channel_id=1, replica_groups=mesh['groups'=2,'kvb'=4,'tp'=4] {'tp'}, dimensions={1}, use_global_device_ids=true | all-gather | bytes 81920 | tf_op jit(solution)/shard_map/all_gather | solution.py:33
  14.3 14.5 %all-gather = bf16[4,4,8192]{2,1,0:T(4,128)(2,1)S(1)} all-gather(bf16[1,4,8192]{2,1,0:T(4,128)(2,1)S(1)} %bitcast.100), channel_id=1, replica_groups=mesh['groups'=2,'kvb'=4,'tp'=4] {'kvb'}, dimensions={0}, use_global_device_ids=true | all-gather | bytes 327680 | tf_op jit(solution)/shard_map/all_gather | solution.py:34
  28.8 0.3 reshape.180
  29.4 7.9 %while.17 = (s32[]{:T(128)}, f32[16,8,8]{0,2,1:T(8,128)S(1)}, f32[16,8,8]{0,2,1:T(8,128)S(1)}, f32[16,8,8,128]{3,0,2,1:T(8,128)S(1)}, s32[]{:T(128)}, /*index=5*...) while((s32[]{:T(128)}, f32[16,8,8]{0,2,1:T(8,128)S(1)}, ...), condition=%wide.region_4.5_spmd.clone.clone, body=%wide.region_0.4_spmd.clone.clone.sunk | while | flops 274516576 | bytes 18212968 | solution.py:82
  29.4 0.7 dynamic_slice.42
  30.3 0.7 fusion.44
  31.1 0.7 dynamic-slice_multiply_fusion.2
  32.0 0.7 add_compare_fusion.2
  32.8 1.7 %constant_dynamic-slice_fusion.5 = (bf16[32,16,1024]{2,1,0:T(8,128)(2,1)S(1)}, bf16[32,16,1024]{2,1,0:T(8,128)(2,1)S(1)}) fusion(bf16[64,16,2048]{2,1,0:T(8,128)(2,1)} %get-tuple-element.348, s32[]{:T(128)S(6)} %select_n.72, s32[]{:T(128)S(6)} %add.157), kind=kLoop, calls=%fused_computation.28.clone.1 | loop fusion | bytes 4194312 | tf_op jit(solution)/shard_map/while/body/slice | solution.py:50
  34.5 0.3 copy.84
  34.8 0.6 fusion.46
  35.4 0.6 fusion.47
  36.1 0.3 copy.85
  36.3 0.9 fusion.48
  37.5 0.6 copy.36
  38.1 12.3 %all-to-all-start = ((f32[16,4,16]{2,1,0:T(4,128)}), f32[16,4,16]{2,1,0:T(4,128)S(1)}, u32[]{:S(2)}, u32[]{:S(2)}) async-start(f32[16,4,16]{2,1,0:T(4,128)} %copy.36), calls=%async_computation | async-start | bytes 65536 | tf_op jit(solution)/shard_map/all_to_all | solution.py:97
  50.4 0.7 dynamic-slice_convert_fusion
  51.3 0.6 copy.41
  52.0 5.1 %all-to-all-done = f32[16,4,16]{2,1,0:T(4,128)S(1)} async-done(((f32[16,4,16]{2,1,0:T(4,128)}), f32[16,4,16]{2,1,0:T(4,128)S(1)}, u32[]{:S(2)}, u32[]{:S(2)}) %all-to-all-start) | async-done | bytes 4128 | tf_op jit(solution)/shard_map/all_to_all | solution.py:97
  57.0 3.5 %all-to-all-start.2 = ((f32[16,4,16]{2,1,0:T(4,128)}), f32[16,4,16]{2,1,0:T(4,128)S(1)}, u32[]{:S(2)}, u32[]{:S(2)}) async-start(f32[16,4,16]{2,1,0:T(4,128)} %copy.41), calls=%async_computation.2 | async-start | bytes 65536 | tf_op jit(solution)/shard_map/all_to_all | solution.py:104
  60.8 0.2 reshape.186
  61.0 1.1 copy.38
  62.2 5.0 %all-to-all-done.2 = f32[16,4,16]{2,1,0:T(4,128)S(1)} async-done(((f32[16,4,16]{2,1,0:T(4,128)}), f32[16,4,16]{2,1,0:T(4,128)S(1)}, u32[]{:S(2)}, u32[]{:S(2)}) %all-to-all-start.2) | async-done | bytes 4128 | tf_op jit(solution)/shard_map/all_to_all | solution.py:104
  67.1 3.6 %all-to-all-start.1 = ((f32[16,4,2048]{2,1,0:T(4,128)}), f32[16,4,2048]{2,1,0:T(4,128)S(1)}, u32[]{:S(2)}, u32[]{:S(2)}) async-start(f32[16,4,2048]{2,1,0:T(4,128)} %bitcast.7), calls=%async_computation.1 | async-start | bytes 1048576 | tf_op jit(solution)/shard_map/all_to_all | solution.py:90
  71.0 0.2 mul.96
  71.2 0.2 mul.97
  71.4 13.5 %all-to-all-done.1 = f32[16,4,2048]{2,1,0:T(4,128)S(1)} async-done(((f32[16,4,2048]{2,1,0:T(4,128)}), f32[16,4,2048]{2,1,0:T(4,128)S(1)}, u32[]{:S(2)}, u32[]{:S(2)}) %all-to-all-start.1) | async-done | bytes 524320 | tf_op jit(solution)/shard_map/all_to_all | solution.py:90
  85.1 13.5 %fusion.24 = f32[4,8192]{1,0:T(4,128)} fusion(bf16[2048,8192]{1,0:T(8,128)(2,1)} %param.20, f32[1,4,16,128]{3,2,1,0:T(8,128)S(1)} %get-tuple-element.225, f32[4,2048]{1,0:T(4,128)S(1)} %multiply_reduce_fusion, f32[1,4,16,128]{3,2,1,0:T(8,128)S(1)} %broadcast_bitcast_fusion.1, f32[1,4,16,128]{3,2,1,0:T(8,128)S(1)} %get-tuple-element.226), kind=kOutput, calls=%fused_computation.41 | convolution fusion | flops 134250496 | bytes 33816576 | tf_op jit(solution)/shard_map/dot_general | solution.py:140
  98.7 30.4 %all-reduce.2.cloned.1.call-done = f32[4,8192]{1,0:T(4,128)} async-done(((f32[4,8192]{1,0:T(4,128)}), f32[4,8192]{1,0:T(4,128)}) %all-reduce.2.cloned.1.call-update) | async-done | bytes 131088 | tf_op jit(solution)/shard_map/psum | solution.py:143
  129.1 0.9 add_convert_fusion
  130.3 0.6 constant_dynamic-slice_fusion.2
  130.9 0.7 multiply_convert_fusion
  (46 shorter events, 2.1 us)
Async XLA Ops:
  29.4 31.2 %copy-start.1 = (bf16[4,2048]{1,0:T(4,128)(2,1)S(1)}, bf16[4,2048]{1,0:T(4,128)(2,1)}, u32[]{:S(2)}) copy-start(bf16[4,2048]{1,0:T(4,128)(2,1)} %param.13) | copy-start | bytes 49156
  38.1 18.9 %all-to-all-start = ((f32[16,4,16]{2,1,0:T(4,128)}), f32[16,4,16]{2,1,0:T(4,128)S(1)}, u32[]{:S(2)}, u32[]{:S(2)}) async-start(f32[16,4,16]{2,1,0:T(4,128)} %copy.36), calls=%async_computation | async-start | bytes 65536 | tf_op jit(solution)/shard_map/all_to_all | solution.py:97
  57.0 10.1 %all-to-all-start.2 = ((f32[16,4,16]{2,1,0:T(4,128)}), f32[16,4,16]{2,1,0:T(4,128)S(1)}, u32[]{:S(2)}, u32[]{:S(2)}) async-start(f32[16,4,16]{2,1,0:T(4,128)} %copy.41), calls=%async_computation.2 | async-start | bytes 65536 | tf_op jit(solution)/shard_map/all_to_all | solution.py:104
  67.1 17.8 %all-to-all-start.1 = ((f32[16,4,2048]{2,1,0:T(4,128)}), f32[16,4,2048]{2,1,0:T(4,128)S(1)}, u32[]{:S(2)}, u32[]{:S(2)}) async-start(f32[16,4,2048]{2,1,0:T(4,128)} %bitcast.7), calls=%async_computation.1 | async-start | bytes 1048576 | tf_op jit(solution)/shard_map/all_to_all | solution.py:90
  70.7 58.4 %all-reduce.2.cloned.1.call-start = ((), (), s32[]{:S(2)}) async-start(), calls=%async_computation.3 | async-start | bytes 262144 | tf_op jit(solution)/shard_map/psum | solution.py:143
  85.1 13.6 %copy-start.2 = (bf16[2048]{0:T(1024)(128)(2,1)S(1)}, bf16[2048]{0:T(1024)(128)(2,1)}, u32[]{:S(2)}) copy-start(bf16[2048]{0:T(1024)(128)(2,1)} %param.21) | copy-start | bytes 12292
  85.1 44.0 %copy-start = (bf16[4,8192]{1,0:T(4,128)(2,1)S(1)}, bf16[4,8192]{1,0:T(4,128)(2,1)}, u32[]{:S(2)}) copy-start(bf16[4,8192]{1,0:T(4,128)(2,1)} %param.12) | copy-start | bytes 196612
Sparse Core Ops, SparseCore 0:
  98.8 30.2 all-reduce.1
where the time goes:
time: 139 us; the launch traced here: 138 us
  waiting for transfers between devices  54 us (39%)
  blocking collectives  21 us (15%)
  starting transfers between devices  19.4 us (14%)
  matrix products  15.1 us (11%)
  between operations  14.9 us (11%)
  local copies, waits for them, and re-layouts  8.16 us (6%)
  other arithmetic  5.66 us (4%)
    psum x1, waiting for transfers between devices, on_device(): summed = lax.psum(projected, 'tp')  30.4 us
    all_gather x1, blocking collectives, on_device(): every = lax.all_gather(wide, 'kvb', axis=0, tiled=True)  14.5 us
    dot_general x1, matrix products, on_device(): jnp.dot(attended, out_weight, preferred_element_type=jnp.float32)  13.5 us
    all_to_all x1, waiting for transfers between devices, on_device(): lax.all_to_all(row_out.reshape(device_total, seq_rep, local_heads * HD),...  13.5 us
    all_to_all x1, starting transfers between devices, on_device(): lax.all_to_all(peak_out.reshape(device_total, seq_rep, local_heads), ('kv...  12.3 us
    all_gather x1, blocking collectives, on_device(): wide = lax.all_gather(queries, 'tp', axis=1, tiled=True)  6.46 us
    all_to_all x1, waiting for transfers between devices, on_device(): lax.all_to_all(peak_out.reshape(device_total, seq_rep, local_heads), ('kv...  5.08 us
    all_to_all x1, waiting for transfers between devices, on_device(): lax.all_to_all(sum_out.reshape(device_total, seq_rep, local_heads), ('kvb...  4.97 us
  transfers between devices with their start and end apart: 4, of which 4 were waited for; matrix products, arithmetic and copies ran while one was open for 3% of the time, Pallas kernels for 0%

commit v1 on v0

--- a/solution.py
+++ b/solution.py
@@ -9,6 +9,16 @@
 BLK = 16
 NEGATIVE = -1e30
 EPSILON = 1e-06
+
+
+def turned_line(x, name, dim):
+    count = lax.axis_size(name)
+    held, tiles = (x, [x])
+    for _ in range(count - 1):
+        held = lax.ppermute(held, name, [(i, (i + 1) % count) for i in range(count)])
+        tiles.insert(0, held)
+    line = jnp.concatenate(tiles, axis=dim)
+    return jnp.roll(line, (lax.axis_index(name) + 1) * x.shape[dim], axis=dim)
 
 
 def on_device(
@@ -31,7 +41,7 @@
     group_size = QH // KVH
     score_scale = HD ** (-0.5)
     wide = lax.all_gather(queries, "tp", axis=1, tiled=True)
-    every = lax.all_gather(wide, "kvb", axis=0, tiled=True)
+    every = turned_line(wide, "kvb", 0)
     seq_total = every.shape[0]
     grouped = every.reshape(seq_total, KVH, group_size, HD)
     pool_size = kv_cache.shape[0]

time: 139 us -> 139 us (level)
  waiting for transfers between devices: 54 us -> 73.9 us
  blocking collectives: 21 us -> 6.59 us
  starting transfers between devices: 19.4 us -> 15.6 us
    ppermute x0 -> x3, waiting for transfers between devices: none -> 16 us  [turned_line(): lax.ppermute(held, name, [(i, (i + 1) % count) for i in range(count)])]
    all_gather x1 -> x0, blocking collectives: 14.5 us -> none  [on_device(): every = lax.all_gather(wide, 'kvb', axis=0, tiled=True)]
    all_to_all x1, starting transfers between devices: 12.3 us -> 6.43 us  [on_device(): lax.all_to_all(peak_out.reshape(device_total, seq_rep, local_heads), ('kv...]
    psum x1, waiting for transfers between devices: 30.4 us -> 34.3 us  [on_device(): summed = lax.psum(projected, 'tp')]
    ppermute x0 -> x3, starting transfers between devices: none -> 2.05 us  [turned_line(): lax.ppermute(held, name, [(i, (i + 1) % count) for i in range(count)])]
  transfers between devices with their start and end apart: 4 -> 7, of which waited for: 4 -> 7; matrix products, arithmetic and copies ran while one was open for 3% -> 3% of each run, Pallas kernels for 0% -> 0%
where the time goes in v1:
time: 139 us; the launch traced here: 138 us
  waiting for transfers between devices  73.9 us (53%)
  starting transfers between devices  15.6 us (11%)
  matrix products  15.1 us (11%)
  between operations  15 us (11%)
  local copies, waits for them, and re-layouts  7.73 us (6%)
  blocking collectives  6.59 us (5%)
  other arithmetic  4.35 us (3%)
    psum x1, waiting for transfers between devices, on_device(): summed = lax.psum(projected, 'tp')  34.3 us
    ppermute x3, waiting for transfers between devices, turned_line(): lax.ppermute(held, name, [(i, (i + 1) % count) for i in range(count)])  16 us
    dot_general x1, matrix products, on_device(): jnp.dot(attended, out_weight, preferred_element_type=jnp.float32)  13.5 us
    all_to_all x1, waiting for transfers between devices, on_device(): lax.all_to_all(row_out.reshape(device_total, seq_rep, local_heads * HD),...  13.5 us
    all_gather x1, blocking collectives, on_device(): wide = lax.all_gather(queries, 'tp', axis=1, tiled=True)  6.59 us
    all_to_all x1, starting transfers between devices, on_device(): lax.all_to_all(peak_out.reshape(device_total, seq_rep, local_heads), ('kv...  6.43 us
    all_to_all x1, waiting for transfers between devices, on_device(): lax.all_to_all(peak_out.reshape(device_total, seq_rep, local_heads), ('kv...  5.08 us
    all_to_all x1, waiting for transfers between devices, on_device(): lax.all_to_all(sum_out.reshape(device_total, seq_rep, local_heads), ('kvb...  4.96 us
  transfers between devices with their start and end apart: 7, of which 7 were waited for; matrix products, arithmetic and copies ran while one was open for 3% of the time, Pallas kernels for 0%

profile of v1, /device:TPU:0, one launch (start us, length us, event | category | flops | bytes accessed | tf_op | source)
XLA Modules:
  0.0 138.4 jit_solution(1293391999844865975)
XLA Ops:
  7.2 6.6 %all_gather.3 = bf16[4,8192]{1,0:T(4,128)(2,1)S(1)} all-gather(bf16[4,2048]{1,0:T(4,128)(2,1)} %param.13), channel_id=1, replica_groups=mesh['groups'=2,'kvb'=4,'tp'=4] {'tp'}, dimensions={1}, use_global_device_ids=true | all-gather | bytes 81920 | tf_op jit(solution)/shard_map/all_gather | solution.py:43
  13.8 2.0 %collective-permute-start = (bf16[4,8192]{1,0:T(4,128)(2,1)S(1)}, bf16[4,8192]{1,0:T(4,128)(2,1)S(1)}, u32[]{:S(2)}, u32[]{:S(2)}) collective-permute-start(bf16[4,8192]{1,0:T(4,128)(2,1)S(1)} %all_gather.3), channel_id=1, source_target_pairs={{0,4},{4,8},{8,12},{12,0},{1,5},{5,9},{9,13},{13,1},{2,6},{6,10},{... | collective-permute-start | bytes 196616 | tf_op jit(solution)/shard_map/ppermute | solution.py:18
  15.8 4.6 %collective-permute-done = bf16[4,8192]{1,0:T(4,128)(2,1)S(1)} collective-permute-done((bf16[4,8192]{1,0:T(4,128)(2,1)S(1)}, bf16[4,8192]{1,0:T(4,128)(2,1)S(1)}, u32[]{:S(2)}, u32[]{:S(2)}) %collective-permute-start) | collective-permute-done | bytes 65568 | tf_op jit(solution)/shard_map/ppermute | solution.py:18
  20.5 6.1 %collective-permute-done.1 = bf16[4,8192]{1,0:T(4,128)(2,1)S(1)} collective-permute-done((bf16[4,8192]{1,0:T(4,128)(2,1)S(1)}, bf16[4,8192]{1,0:T(4,128)(2,1)S(1)}, u32[]{:S(2)}, u32[]{:S(2)}) %collective-permute-start.1) | collective-permute-done | bytes 65568 | tf_op jit(solution)/shard_map/ppermute | solution.py:18
  27.2 5.4 %collective-permute-done.2 = bf16[4,8192]{1,0:T(4,128)(2,1)S(1)} collective-permute-done((bf16[4,8192]{1,0:T(4,128)(2,1)S(1)}, bf16[4,8192]{1,0:T(4,128)(2,1)S(1)}, u32[]{:S(2)}, u32[]{:S(2)}) %collective-permute-start.2) | collective-permute-done | bytes 65568 | tf_op jit(solution)/shard_map/ppermute | solution.py:18
  32.6 0.3 concatenate.6
  33.4 5.9 %while.17 = (s32[]{:T(128)}, f32[16,8,8]{0,2,1:T(8,128)S(1)}, f32[16,8,8]{0,2,1:T(8,128)S(1)}, f32[16,8,8,128]{3,0,2,1:T(8,128)S(1)}, s32[]{:T(128)}, /*index=5*...) while((s32[]{:T(128)}, f32[16,8,8]{0,2,1:T(8,128)S(1)}, ...), condition=%wide.region_4.5_spmd.clone.clone, body=%wide.region_0.4_spmd.clone.clone.sunk | while | flops 274516576 | bytes 18212968 | solution.py:92
  34.0 0.7 add_compare_fusion.2
  34.8 1.7 %constant_dynamic-slice_fusion.5 = (bf16[32,16,1024]{2,1,0:T(8,128)(2,1)S(1)}, bf16[32,16,1024]{2,1,0:T(8,128)(2,1)S(1)}) fusion(bf16[64,16,2048]{2,1,0:T(8,128)(2,1)} %get-tuple-element.348, s32[]{:T(128)S(6)} %select_n.86, s32[]{:T(128)S(6)} %add.173), kind=kLoop, calls=%fused_computation.28.clone.1 | loop fusion | bytes 4194312 | tf_op jit(solution)/shard_map/while/body/slice | solution.py:60
  36.5 0.3 copy.85
  36.8 0.6 fusion.46
  37.4 0.6 fusion.47
  38.1 0.3 copy.86
  38.4 0.9 fusion.48
  39.5 0.6 copy.36
  40.1 6.4 %all-to-all-start = ((f32[16,4,16]{2,1,0:T(4,128)}), f32[16,4,16]{2,1,0:T(4,128)S(1)}, u32[]{:S(2)}, u32[]{:S(2)}) async-start(f32[16,4,16]{2,1,0:T(4,128)} %copy.36), calls=%async_computation | async-start | bytes 65536 | tf_op jit(solution)/shard_map/all_to_all | solution.py:107
  46.6 0.7 dynamic-slice_convert_fusion
  47.5 0.6 copy.41
  48.1 5.1 %all-to-all-done = f32[16,4,16]{2,1,0:T(4,128)S(1)} async-done(((f32[16,4,16]{2,1,0:T(4,128)}), f32[16,4,16]{2,1,0:T(4,128)S(1)}, u32[]{:S(2)}, u32[]{:S(2)}) %all-to-all-start) | async-done | bytes 4128 | tf_op jit(solution)/shard_map/all_to_all | solution.py:107
  53.2 3.5 %all-to-all-start.2 = ((f32[16,4,16]{2,1,0:T(4,128)}), f32[16,4,16]{2,1,0:T(4,128)S(1)}, u32[]{:S(2)}, u32[]{:S(2)}) async-start(f32[16,4,16]{2,1,0:T(4,128)} %copy.41), calls=%async_computation.2 | async-start | bytes 65536 | tf_op jit(solution)/shard_map/all_to_all | solution.py:114
  57.0 0.2 reshape.186
  57.2 1.1 copy.38
  58.3 5.0 %all-to-all-done.2 = f32[16,4,16]{2,1,0:T(4,128)S(1)} async-done(((f32[16,4,16]{2,1,0:T(4,128)}), f32[16,4,16]{2,1,0:T(4,128)S(1)}, u32[]{:S(2)}, u32[]{:S(2)}) %all-to-all-start.2) | async-done | bytes 4128 | tf_op jit(solution)/shard_map/all_to_all | solution.py:114
  63.3 3.6 %all-to-all-start.1 = ((f32[16,4,2048]{2,1,0:T(4,128)}), f32[16,4,2048]{2,1,0:T(4,128)S(1)}, u32[]{:S(2)}, u32[]{:S(2)}) async-start(f32[16,4,2048]{2,1,0:T(4,128)} %bitcast.6), calls=%async_computation.1 | async-start | bytes 1048576 | tf_op jit(solution)/shard_map/all_to_all | solution.py:100
  67.1 0.2 mul.100
  67.3 0.2 mul.101
  67.6 13.5 %all-to-all-done.1 = f32[16,4,2048]{2,1,0:T(4,128)S(1)} async-done(((f32[16,4,2048]{2,1,0:T(4,128)}), f32[16,4,2048]{2,1,0:T(4,128)S(1)}, u32[]{:S(2)}, u32[]{:S(2)}) %all-to-all-start.1) | async-done | bytes 524320 | tf_op jit(solution)/shard_map/all_to_all | solution.py:100
  81.3 13.5 %fusion.24 = f32[4,8192]{1,0:T(4,128)} fusion(bf16[2048,8192]{1,0:T(8,128)(2,1)} %param.20, f32[1,4,16,128]{3,2,1,0:T(8,128)S(1)} %get-tuple-element.225, f32[4,2048]{1,0:T(4,128)S(1)} %multiply_reduce_fusion, f32[1,4,16,128]{3,2,1,0:T(8,128)S(1)} %broadcast_bitcast_fusion.1, f32[1,4,16,128]{3,2,1,0:T(8,128)S(1)} %get-tuple-element.226), kind=kOutput, calls=%fused_computation.42 | convolution fusion | flops 134250496 | bytes 33816576 | tf_op jit(solution)/shard_map/dot_general | solution.py:150
  94.8 34.3 %all-reduce.2.cloned.1.call-done = f32[4,8192]{1,0:T(4,128)} async-done(((f32[4,8192]{1,0:T(4,128)}), f32[4,8192]{1,0:T(4,128)}) %all-reduce.2.cloned.1.call-update) | async-done | bytes 131088 | tf_op jit(solution)/shard_map/psum | solution.py:153
  129.1 0.9 add_convert_fusion
  130.3 0.6 constant_dynamic-slice_fusion.2
  130.9 0.7 multiply_convert_fusion
  (59 shorter events, 2.5 us)
Async XLA Ops:
  7.2 26.2 %copy-start.2 = (s32[16]{0:T(128)S(1)}, s32[16]{0:T(128)}, u32[]{:S(2)}) copy-start(s32[16]{0:T(128)} %param.16) | copy-start | bytes 196
  7.2 26.2 %copy-start.4 = (s32[64]{0:T(128)S(1)}, s32[64]{0:T(128)}, u32[]{:S(2)}) copy-start(s32[64]{0:T(128)} %param.17) | copy-start | bytes 772
  7.2 26.2 %copy-start.5 = (s32[64]{0:T(128)S(1)}, s32[64]{0:T(128)}, u32[]{:S(2)}) copy-start(s32[64]{0:T(128)} %param.18) | copy-start | bytes 772
  13.8 6.7 %collective-permute-start = (bf16[4,8192]{1,0:T(4,128)(2,1)S(1)}, bf16[4,8192]{1,0:T(4,128)(2,1)S(1)}, u32[]{:S(2)}, u32[]{:S(2)}) collective-permute-start(bf16[4,8192]{1,0:T(4,128)(2,1)S(1)} %all_gather.3), channel_id=1, source_target_pairs={{0,4},{4,8},{8,12},{12,0},{1,5},{5,9},{9,13},{13,1},{2,6},{6,10},{... | collective-permute-start | bytes 196616 | tf_op jit(solution)/shard_map/ppermute | solution.py:18
  20.5 6.1 %collective-permute-start.1 = (bf16[4,8192]{1,0:T(4,128)(2,1)S(1)}, bf16[4,8192]{1,0:T(4,128)(2,1)S(1)}, u32[]{:S(2)}, u32[]{:S(2)}) collective-permute-start(bf16[4,8192]{1,0:T(4,128)(2,1)S(1)} %collective-permute-done), channel_id=1, source_target_pairs={{0,4},{4,8},{8,12},{12,0},{1,5},{5,9},{9,13},{13,1},{2,6},{6,10},{... | collective-permute-start | bytes 196616 | tf_op jit(solution)/shard_map/ppermute | solution.py:18
  26.5 6.1 %collective-permute-start.2 = (bf16[4,8192]{1,0:T(4,128)(2,1)S(1)}, bf16[4,8192]{1,0:T(4,128)(2,1)S(1)}, u32[]{:S(2)}, u32[]{:S(2)}) collective-permute-start(bf16[4,8192]{1,0:T(4,128)(2,1)S(1)} %collective-permute-done.1), channel_id=1, source_target_pairs={{0,4},{4,8},{8,12},{12,0},{1,5},{5,9},{9,13},{13,1},{2,6},{6,10},{... | collective-permute-start | bytes 196616 | tf_op jit(solution)/shard_map/ppermute | solution.py:18
  33.4 23.3 %copy-start.1 = (bf16[4,2048]{1,0:T(4,128)(2,1)S(1)}, bf16[4,2048]{1,0:T(4,128)(2,1)}, u32[]{:S(2)}) copy-start(bf16[4,2048]{1,0:T(4,128)(2,1)} %param.13) | copy-start | bytes 49156
  40.1 13.1 %all-to-all-start = ((f32[16,4,16]{2,1,0:T(4,128)}), f32[16,4,16]{2,1,0:T(4,128)S(1)}, u32[]{:S(2)}, u32[]{:S(2)}) async-start(f32[16,4,16]{2,1,0:T(4,128)} %copy.36), calls=%async_computation | async-start | bytes 65536 | tf_op jit(solution)/shard_map/all_to_all | solution.py:107
  53.2 10.1 %all-to-all-start.2 = ((f32[16,4,16]{2,1,0:T(4,128)}), f32[16,4,16]{2,1,0:T(4,128)S(1)}, u32[]{:S(2)}, u32[]{:S(2)}) async-start(f32[16,4,16]{2,1,0:T(4,128)} %copy.41), calls=%async_computation.2 | async-start | bytes 65536 | tf_op jit(solution)/shard_map/all_to_all | solution.py:114
  63.3 17.8 %all-to-all-start.1 = ((f32[16,4,2048]{2,1,0:T(4,128)}), f32[16,4,2048]{2,1,0:T(4,128)S(1)}, u32[]{:S(2)}, u32[]{:S(2)}) async-start(f32[16,4,2048]{2,1,0:T(4,128)} %bitcast.6), calls=%async_computation.1 | async-start | bytes 1048576 | tf_op jit(solution)/shard_map/all_to_all | solution.py:100
  66.9 62.3 %all-reduce.2.cloned.1.call-start = ((), (), s32[]{:S(2)}) async-start(), calls=%async_computation.3 | async-start | bytes 262144 | tf_op jit(solution)/shard_map/psum | solution.py:153
  81.2 13.6 %copy-start.3 = (bf16[2048]{0:T(1024)(128)(2,1)S(1)}, bf16[2048]{0:T(1024)(128)(2,1)}, u32[]{:S(2)}) copy-start(bf16[2048]{0:T(1024)(128)(2,1)} %param.21) | copy-start | bytes 12292
  81.2 47.9 %copy-start = (bf16[4,8192]{1,0:T(4,128)(2,1)S(1)}, bf16[4,8192]{1,0:T(4,128)(2,1)}, u32[]{:S(2)}) copy-start(bf16[4,8192]{1,0:T(4,128)(2,1)} %param.12) | copy-start | bytes 196612
Sparse Core Ops, SparseCore 0:
  94.9 34.1 all-reduce.1
